TPU v7x, 32 devices: a whole 2x2x4 slice. The times are simulated.
32 devices in a mesh: lat: 4 (over y, x), lon: 8 (over z, core).
Axes of the slice: x: 2, y: 2, z: 4, core: 2. Of those that a mesh axis runs over, the one named last changes fastest.
Arguments:
- forcing: float32 [256, 2048], P('lat', 'lon'), may hold values from -32 to 32
- depth_east: float32 [256, 2048], P('lat', 'lon'), may hold values from 0.25 to 4
- depth_north: float32 [256, 2048], P('lat', 'lon'), may hold values from 0.25 to 4
- surface_term: float32 [256, 2048], P('lat', 'lon'), may hold values from 0.02 to 0.5
- ocean_mask: int32 [256, 2048], P('lat', 'lon'), may hold values 0 or 1
- cost_weights: float32 [8, 256, 2048], P(None, 'lat', 'lon'), may hold values from -6 to 6
Outputs:
- forcing_adjoint: float32 [8, 256, 2048], P(None, 'lat', 'lon')
- east_gradient: float32 [8, 256, 2048], P(None, 'lat', 'lon')
- north_gradient: float32 [8, 256, 2048], P(None, 'lat', 'lon')
Inputs may be any that keep to these rules, and one draw needn't show every extreme that they name: `ocean_mask`: 1 marks an ocean cell, 0 a land cell.
All inputs are finite; a program needn't handle non-finite values. No bound on the sum of `ocean_mask` on one device may be relied on, other than what follows from the above.
Results may differ from a plain program's by a relative error of at most 0.00018.
Values sent between devices are 32-bit elements; how exact they have to be, the bound alone decides.
A program may use at most 64 MiB of HBM per device.

v0:
```python
import jax
import jax.numpy as jnp
from jax import lax
from jax.sharding import PartitionSpec as P

ITERS = 6


def padded_2(block, sides, width, periodic):
    for axis, dim in sides:
        count = lax.axis_size(axis)
        forward = [(i, i + 1) for i in range(count - 1)]
        if periodic:
            forward.append((count - 1, 0))
        backward = [(target, source) for source, target in forward]
        low = lax.ppermute(
            lax.slice_in_dim(block, block.shape[dim] - width, None, axis=dim), axis, forward
        )
        high = lax.ppermute(lax.slice_in_dim(block, 0, width, axis=dim), axis, backward)
        block = jnp.concatenate([low, block, high], axis=dim)
    return block


def shifted(value, axis, steps):
    count = lax.axis_size(axis)
    pairs = [(source, (source + steps) % count) for source in range(count)]
    return lax.ppermute(value, axis, pairs)


def shifted_2(block, axis, distance):
    devices = range(lax.axis_size(axis))
    route = [(i - distance, i) for i in devices if i - distance in devices]
    return lax.ppermute(block, axis, route)


def widen_coefs(stacked):
    wider = padded_2(stacked, (("lon", 2),), 1, True)
    return padded_2(wider, (("lat", 1),), 1, False)


def widen_precond(field):
    wider = padded_2(field, (("lon", 1),), 1, True)
    return padded_2(wider, (("lat", 0),), 1, False)


def widen_image(stack):
    wider = padded_2(stack, (("lon", 2),), 1, True)
    return padded_2(wider, (("lat", 1),), 1, False)


def operate(padded, coefs):
    base, east_face, west_face, north_face, south_face = coefs
    centre = padded[..., 1:-1, 1:-1]
    return (
        base * centre
        + east_face * (centre - padded[..., 1:-1, 2:])
        + west_face * (centre - padded[..., 1:-1, :-2])
        + north_face * (centre - padded[..., 2:, 1:-1])
        + south_face * (centre - padded[..., :-2, 1:-1])
    )


def smoothed_terms(residual, diagonal, coefs):
    precond = residual / diagonal
    prec_pad = widen_precond(precond)
    smooth = operate(prec_pad, coefs)
    norm_value, delta = lax.psum(
        (jnp.sum(residual * precond), jnp.sum(precond * smooth)), ("lat", "lon")
    )
    return (prec_pad, smooth, norm_value, delta)


def body(forcing, depth_east, depth_north, surface_term, ocean_mask, cost_weights):
    stacked = jnp.stack([ocean_mask.astype(jnp.float32), depth_east, depth_north])
    padded = widen_coefs(stacked)
    wet = padded[0]
    east_all = padded[1][:, :-1] * wet[:, :-1] * wet[:, 1:]
    north_all = padded[2][:-1, :] * wet[:-1, :] * wet[1:, :]
    east_face = east_all[1:-1, 1:]
    west_face = east_all[1:-1, :-1]
    north_face = north_all[1:, 1:-1]
    south_face = north_all[:-1, 1:-1]
    ocean = wet[1:-1, 1:-1]
    mask_east = ocean * wet[1:-1, 2:]
    mask_north = ocean * wet[2:, 1:-1]
    base = ocean * surface_term + 1.0 - ocean
    diagonal = base + east_face + west_face + north_face + south_face
    coefs = (base, east_face, west_face, north_face, south_face)
    residual = forcing
    padded_dirs = []
    images = []
    residuals = []
    alphas = []
    betas = []
    pairs = []
    prec_pad, smooth, norm_first, delta = smoothed_terms(residual, diagonal, coefs)
    norms = [norm_first]
    alpha = norm_first / delta
    dir_pad = prec_pad
    image = smooth
    for step in range(ITERS):
        padded_dirs.append(dir_pad)
        images.append(image)
        alphas.append(alpha)
        pairs.append(norms[-1] / alpha)
        residual = residual - alpha * image
        if step < ITERS - 1:
            residuals.append(residual)
            prec_pad, smooth, norm_next, delta = smoothed_terms(residual, diagonal, coefs)
            beta = norm_next / norms[-1]
            alpha = norm_next / (delta - beta * norm_next / alpha)
            dir_pad = prec_pad + beta * dir_pad
            image = smooth + beta * image
            norms.append(norm_next)
            betas.append(beta)
    projections = lax.psum(
        jnp.stack(
            [
                jnp.sum(cost_weights * padded_dirs[step][1:-1, 1:-1], axis=(1, 2))
                for step in range(ITERS)
            ]
        ),
        ("lat", "lon"),
    )
    last = ITERS - 1
    dir_pad = padded_dirs[last]
    inner_dir = dir_pad[1:-1, 1:-1]
    alpha_bar = projections[last]
    norm_bar = alpha_bar / pairs[last]
    pair_bar = -alpha_bar * alphas[last] / pairs[last]
    scale = pair_bar[:, None, None]
    dir_bar = alphas[last] * cost_weights + 2.0 * scale * images[last]
    east_diff = inner_dir - dir_pad[1:-1, 2:]
    north_diff = inner_dir - dir_pad[2:, 1:-1]
    east_sum = scale * (east_diff * east_diff)
    north_sum = scale * (north_diff * north_diff)
    res_bar = jnp.zeros_like(cost_weights)
    depth_bar = jnp.zeros_like(cost_weights)
    for step in range(ITERS - 2, -1, -1):
        dir_pad = padded_dirs[step]
        inner_dir = dir_pad[1:-1, 1:-1]
        image = images[step]
        resid_next = residuals[step]
        precond_next = resid_next / diagonal
        scaled = dir_bar / diagonal
        beta_term = lax.psum(jnp.sum(dir_bar * inner_dir, axis=(1, 2)), ("lat", "lon"))
        norm_next_bar = norm_bar + beta_term / norms[step]
        res_new = res_bar + scaled + 2.0 * norm_next_bar[:, None, None] * precond_next
        alpha_bar = projections[step] - lax.psum(
            jnp.sum(res_new * image, axis=(1, 2)), ("lat", "lon")
        )
        pre_bar = dir_bar + norm_next_bar[:, None, None] * resid_next
        depth_bar = depth_bar - pre_bar * precond_next / diagonal
        norm_bar = (
            -beta_term * norms[step + 1] / (norms[step] * norms[step]) + alpha_bar / pairs[step]
        )
        pair_bar = -alpha_bar * alphas[step] / pairs[step]
        scale = pair_bar[:, None, None]
        image_pad = widen_image(-alphas[step] * res_new + scale * inner_dir)
        dir_bar = (
            betas[step] * dir_bar
            + alphas[step] * cost_weights
            + scale * image
            + operate(image_pad, coefs)
        )
        centre = image_pad[:, 1:-1, 1:-1]
        east_sum = east_sum + (centre - image_pad[:, 1:-1, 2:]) * (inner_dir - dir_pad[1:-1, 2:])
        north_sum = north_sum + (centre - image_pad[:, 2:, 1:-1]) * (inner_dir - dir_pad[2:, 1:-1])
        res_bar = res_new
    precond_first = forcing / diagonal
    pre_bar = dir_bar + norm_bar[:, None, None] * forcing
    forcing_adjoint = res_bar + dir_bar / diagonal + 2.0 * norm_bar[:, None, None] * precond_first
    depth_bar = depth_bar - pre_bar * precond_first / diagonal
    east_column = shifted(depth_bar[:, :, :1], "lon", -1)
    north_row = shifted_2(depth_bar[:, :1, :], "lat", -1)
    depth_eastward = jnp.concatenate([depth_bar[:, :, 1:], east_column], axis=2)
    depth_northward = jnp.concatenate([depth_bar[:, 1:, :], north_row], axis=1)
    east_gradient = mask_east * (east_sum + depth_bar + depth_eastward)
    north_gradient = mask_north * (north_sum + depth_bar + depth_northward)
    return (forcing_adjoint, east_gradient, north_gradient)


def solution(mesh):
    return jax.shard_map(
        body,
        mesh=mesh,
        in_specs=(
            P("lat", "lon"),
            P("lat", "lon"),
            P("lat", "lon"),
            P("lat", "lon"),
            P("lat", "lon"),
            P(None, "lat", "lon"),
        ),
        out_specs=(P(None, "lat", "lon"), P(None, "lat", "lon"), P(None, "lat", "lon")),
        check_vma=False,
    )
```

profile of v0, /device:TPU:31, one launch (start us, length us, event | category | flops | bytes accessed | tf_op | source)
XLA Modules:
  0.0 978.9 jit_solution(14568244211439639987)
XLA Ops:
  3.8 4.2 collective-permute-done.1
  30.8 41.1 %all-reduce.5 = (f32[]{:T(128)}, f32[]{:T(128)}) all-reduce(f32[]{:T(128)} %get-tuple-element.20, f32[]{:T(128)} %get-tuple-element.19), channel_id=1, replica_groups=mesh['lat'=4,'lon'=8] {'lat','lon'}, use_global_device_ids=true, to_apply=%region_1.0 | all-reduce | flops 2 | bytes 16 | tf_op jit(solution)/shard_map/psum | solution.py:67
  87.5 41.0 %all-reduce.4 = (f32[]{:T(128)}, f32[]{:T(128)}) all-reduce(f32[]{:T(128)} %get-tuple-element.18, f32[]{:T(128)} %get-tuple-element.17), channel_id=1, replica_groups=mesh['lat'=4,'lon'=8] {'lat','lon'}, use_global_device_ids=true, to_apply=%region_5.0 | all-reduce | flops 2 | bytes 16 | tf_op jit(solution)/shard_map/psum | solution.py:67
  147.0 40.9 %all-reduce.3 = (f32[]{:T(128)}, f32[]{:T(128)}) all-reduce(f32[]{:T(128)} %get-tuple-element.16, f32[]{:T(128)} %get-tuple-element.15), channel_id=1, replica_groups=mesh['lat'=4,'lon'=8] {'lat','lon'}, use_global_device_ids=true, to_apply=%region_9.0 | all-reduce | flops 2 | bytes 16 | tf_op jit(solution)/shard_map/psum | solution.py:67
  205.9 40.9 %all-reduce.2 = (f32[]{:T(128)}, f32[]{:T(128)}) all-reduce(f32[]{:T(128)} %get-tuple-element.14, f32[]{:T(128)} %get-tuple-element.13), channel_id=1, replica_groups=mesh['lat'=4,'lon'=8] {'lat','lon'}, use_global_device_ids=true, to_apply=%region_13.0 | all-reduce | flops 2 | bytes 16 | tf_op jit(solution)/shard_map/psum | solution.py:67
  264.7 40.9 %all-reduce.1 = (f32[]{:T(128)}, f32[]{:T(128)}) all-reduce(f32[]{:T(128)} %get-tuple-element.12, f32[]{:T(128)} %get-tuple-element.11), channel_id=1, replica_groups=mesh['lat'=4,'lon'=8] {'lat','lon'}, use_global_device_ids=true, to_apply=%region_17.0 | all-reduce | flops 2 | bytes 16 | tf_op jit(solution)/shard_map/psum | solution.py:67
  323.3 41.0 %psum.171 = f32[]{:T(128)} all-reduce(f32[]{:T(128)} %get-tuple-element.10), channel_id=1, replica_groups=mesh['lat'=4,'lon'=8] {'lat','lon'}, use_global_device_ids=true, to_apply=%region_21.0 | all-reduce | flops 1 | bytes 8 | tf_op jit(solution)/shard_map/psum | solution.py:67
  370.4 42.2 %all-reduce = (f32[6,8]{1,0:T(8,128)S(1)}, f32[]{:T(128)}) all-reduce(f32[6,8]{1,0:T(8,128)S(1)} %stack.43, f32[]{:T(128)} %get-tuple-element.9), channel_id=1, replica_groups=mesh['lat'=4,'lon'=8] {'lat','lon'}, use_global_device_ids=true, to_apply=%region_30.0 | all-reduce | flops 49 | bytes 392 | tf_op jit(solution)/shard_map/psum | solution.py:116
  416.8 38.5 %psum.174 = f32[8]{0:T(128)S(1)} all-reduce(f32[8]{0:T(128)S(1)} %multiply_reduce_fusion.9), channel_id=1, replica_groups=mesh['lat'=4,'lon'=8] {'lat','lon'}, use_global_device_ids=true, to_apply=%region_32.0 | all-reduce | flops 8 | bytes 64 | tf_op jit(solution)/shard_map/psum | solution.py:146
  456.7 41.6 %psum.175 = f32[8]{0:T(128)S(1)} all-reduce(f32[8]{0:T(128)S(1)} %get-tuple-element.61), channel_id=1, replica_groups=mesh['lat'=4,'lon'=8] {'lat','lon'}, use_global_device_ids=true, to_apply=%region_34.0 | all-reduce | flops 8 | bytes 64 | tf_op jit(solution)/shard_map/psum | solution.py:149
  503.3 6.8 collective-permute-done.28
  521.9 38.7 %psum.176 = f32[8]{0:T(128)S(1)} all-reduce(f32[8]{0:T(128)S(1)} %copy-done.108), channel_id=1, replica_groups=mesh['lat'=4,'lon'=8] {'lat','lon'}, use_global_device_ids=true, to_apply=%region_36.0 | all-reduce | flops 8 | bytes 64 | tf_op jit(solution)/shard_map/psum | solution.py:146
  563.4 41.8 %psum.177 = f32[8]{0:T(128)S(1)} all-reduce(f32[8]{0:T(128)S(1)} %get-tuple-element.55), channel_id=1, replica_groups=mesh['lat'=4,'lon'=8] {'lat','lon'}, use_global_device_ids=true, to_apply=%region_38.0 | all-reduce | flops 8 | bytes 64 | tf_op jit(solution)/shard_map/psum | solution.py:149
  610.3 6.7 collective-permute-done.32
  628.4 38.9 %psum.178 = f32[8]{0:T(128)} all-reduce(f32[8]{0:T(128)} %get-tuple-element.53), channel_id=1, replica_groups=mesh['lat'=4,'lon'=8] {'lat','lon'}, use_global_device_ids=true, to_apply=%region_40.0 | all-reduce | flops 8 | bytes 64 | tf_op jit(solution)/shard_map/psum | solution.py:146
  672.8 41.8 %psum.179 = f32[8]{0:T(128)S(1)} all-reduce(f32[8]{0:T(128)S(1)} %copy-done.107), channel_id=1, replica_groups=mesh['lat'=4,'lon'=8] {'lat','lon'}, use_global_device_ids=true, to_apply=%region_42.0 | all-reduce | flops 8 | bytes 64 | tf_op jit(solution)/shard_map/psum | solution.py:149
  720.7 6.8 collective-permute-done.36
  741.1 38.3 %psum.180 = f32[8]{0:T(128)S(1)} all-reduce(f32[8]{0:T(128)S(1)} %copy-done.109), channel_id=1, replica_groups=mesh['lat'=4,'lon'=8] {'lat','lon'}, use_global_device_ids=true, to_apply=%region_44.0 | all-reduce | flops 8 | bytes 64 | tf_op jit(solution)/shard_map/psum | solution.py:146
  783.9 41.5 %psum.181 = f32[8]{0:T(128)S(1)} all-reduce(f32[8]{0:T(128)S(1)} %get-tuple-element.43), channel_id=1, replica_groups=mesh['lat'=4,'lon'=8] {'lat','lon'}, use_global_device_ids=true, to_apply=%region_46.0 | all-reduce | flops 8 | bytes 64 | tf_op jit(solution)/shard_map/psum | solution.py:149
  831.4 6.7 collective-permute-done.40
  851.8 39.1 %psum.182 = f32[8]{0:T(128)} all-reduce(f32[8]{0:T(128)} %get-tuple-element.41), channel_id=1, replica_groups=mesh['lat'=4,'lon'=8] {'lat','lon'}, use_global_device_ids=true, to_apply=%region_48.0 | all-reduce | flops 8 | bytes 64 | tf_op jit(solution)/shard_map/psum | solution.py:146
  896.1 42.2 %psum.183 = f32[8]{0:T(128)} all-reduce(f32[8]{0:T(128)} %get-tuple-element.37), channel_id=1, replica_groups=mesh['lat'=4,'lon'=8] {'lat','lon'}, use_global_device_ids=true, to_apply=%region_50.0 | all-reduce | flops 8 | bytes 64 | tf_op jit(solution)/shard_map/psum | solution.py:149
  944.7 6.8 collective-permute-done.44
  967.5 5.4 collective-permute-done.48
  (396 shorter events, 207.5 us)
Async XLA Ops:
  2.2 5.8 collective-permute-start.1
  8.1 5.3 collective-permute-start.2
  73.4 5.7 collective-permute-start.8
  133.1 5.7 collective-permute-start.12
  192.0 5.6 collective-permute-start.16
  250.7 5.7 collective-permute-start.20
  309.4 5.7 collective-permute-start.24
  499.7 10.4 %collective-permute-start.28 = (f32[8,64,1]{2,1,0:T(8,128)S(1)}, f32[8,64,1]{2,1,0:T(8,128)S(1)}, u32[]{:S(2)}, u32[]{:S(2)}) collective-permute-start(f32[8,64,1]{2,1,0:T(8,128)S(1)} %get-tuple-element.114), channel_id=1, source_target_pairs={{1,0},{2,1},{3,2},{4,3},{5,4},{6,5},{7,6},{0,7},{9,8},{10,9},{11,1... | collective-permute-start | bytes 6152 | tf_op jit(solution)/shard_map/ppermute | solution.py:19
  500.9 9.1 collective-permute-start.29
  510.2 6.5 collective-permute-start.30
  606.7 10.3 %collective-permute-start.32 = (f32[8,64,1]{2,1,0:T(8,128)S(1)}, f32[8,64,1]{2,1,0:T(8,128)S(1)}, u32[]{:S(2)}, u32[]{:S(2)}) collective-permute-start(f32[8,64,1]{2,1,0:T(8,128)S(1)} %get-tuple-element.112), channel_id=1, source_target_pairs={{1,0},{2,1},{3,2},{4,3},{5,4},{6,5},{7,6},{0,7},{9,8},{10,9},{11,1... | collective-permute-start | bytes 6152 | tf_op jit(solution)/shard_map/ppermute | solution.py:19
  607.7 9.3 collective-permute-start.33
  617.9 6.6 collective-permute-start.34
  717.1 10.4 %collective-permute-start.36 = (f32[8,64,1]{2,1,0:T(8,128)S(1)}, f32[8,64,1]{2,1,0:T(8,128)S(1)}, u32[]{:S(2)}, u32[]{:S(2)}) collective-permute-start(f32[8,64,1]{2,1,0:T(8,128)S(1)} %get-tuple-element.110), channel_id=1, source_target_pairs={{1,0},{2,1},{3,2},{4,3},{5,4},{6,5},{7,6},{0,7},{9,8},{10,9},{11,1... | collective-permute-start | bytes 6152 | tf_op jit(solution)/shard_map/ppermute | solution.py:19
  718.2 9.3 collective-permute-start.37
  728.3 7.2 collective-permute-start.38
  827.8 10.3 %collective-permute-start.40 = (f32[8,64,1]{2,1,0:T(8,128)S(1)}, f32[8,64,1]{2,1,0:T(8,128)S(1)}, u32[]{:S(2)}, u32[]{:S(2)}) collective-permute-start(f32[8,64,1]{2,1,0:T(8,128)S(1)} %get-tuple-element.108), channel_id=1, source_target_pairs={{1,0},{2,1},{3,2},{4,3},{5,4},{6,5},{7,6},{0,7},{9,8},{10,9},{11,1... | collective-permute-start | bytes 6152 | tf_op jit(solution)/shard_map/ppermute | solution.py:19
  829.0 9.2 collective-permute-start.41
  839.0 9.1 collective-permute-start.42
  842.4 5.7 collective-permute-start.43
  941.1 10.4 %collective-permute-start.44 = (f32[8,64,1]{2,1,0:T(8,128)S(1)}, f32[8,64,1]{2,1,0:T(8,128)S(1)}, u32[]{:S(2)}, u32[]{:S(2)}) collective-permute-start(f32[8,64,1]{2,1,0:T(8,128)S(1)} %get-tuple-element.106), channel_id=1, source_target_pairs={{1,0},{2,1},{3,2},{4,3},{5,4},{6,5},{7,6},{0,7},{9,8},{10,9},{11,1... | collective-permute-start | bytes 6152 | tf_op jit(solution)/shard_map/ppermute | solution.py:19
  942.1 9.3 collective-permute-start.45
  961.3 14.4 %collective-permute-start.49 = (f32[8,1,256]{2,1,0:T(1,128)S(1)}, f32[8,1,256]{2,1,0:T(1,128)S(1)}, u32[]{:S(2)}, u32[]{:S(2)}) collective-permute-start(f32[8,1,256]{2,1,0:T(1,128)S(1)} %slice.651), channel_id=1, source_target_pairs={{8,0},{16,8},{24,16},{9,1},{17,9},{25,17},{10,2},{18,10},{26,18},{... | collective-permute-start | bytes 24584 | tf_op jit(solution)/shard_map/ppermute | solution.py:33
  965.1 7.8 collective-permute-start.48
  (136 other events, 5179.7 us)
where the time goes:
time: 984 us; the launch traced here: 979 us
  blocking collectives  691 us (70%)
  starting transfers between devices  102 us (10%)
  waiting for transfers between devices  79.1 us (8%)
  other arithmetic  58.4 us (6%)
  between operations  37.4 us (4%)
  local copies, waits for them, and re-layouts  11.5 us (1%)
    psum x6, blocking collectives, smoothed_terms(): lax.psum((jnp.sum(residual * precond), jnp.sum(precond * smooth)), ('lat'...  246 us
    psum x5, blocking collectives, body(): lax.psum(jnp.sum(res_new * image, axis=(1, 2)), ('lat', 'lon'))  209 us
    psum x5, blocking collectives, body(): lax.psum(jnp.sum(dir_bar * inner_dir, axis=(1, 2)), ('lat', 'lon'))  193 us
    ppermute x24, starting transfers between devices, padded_2(): lax.ppermute(lax.slice_in_dim(block, 0, width, axis=dim), axis, backward)  58.6 us
    ppermute x24, waiting for transfers between devices, padded_2(): lax.ppermute(lax.slice_in_dim(block, 0, width, axis=dim), axis, backward)  48 us
    psum x1, blocking collectives, body(): lax.psum(jnp.stack([jnp.sum(cost_weights * padded_dirs[step][1:-1, 1:-1],...  42.2 us
    ppermute x24, starting transfers between devices, padded_2(): lax.ppermute(lax.slice_in_dim(block, block.shape[dim] - width, None, axis...  38.3 us
    ppermute x24, waiting for transfers between devices, padded_2(): lax.ppermute(lax.slice_in_dim(block, block.shape[dim] - width, None, axis...  25.6 us
  transfers between devices with their start and end apart: 50, of which 25 were waited for; matrix products, arithmetic and copies ran while one was open for 0% of the time, Pallas kernels for 0%

commit v1 on v0

--- a/solution.py
+++ b/solution.py
@@ -65,7 +65,7 @@
     prec_pad = widen_precond(precond)
     smooth = operate(prec_pad, coefs)
     norm_value, delta = lax.psum(
-        (jnp.sum(residual * precond), jnp.sum(precond * smooth)), ("lat", "lon")
+        lax.psum((jnp.sum(residual * precond), jnp.sum(precond * smooth)), "lat"), "lon"
     )
     return (prec_pad, smooth, norm_value, delta)
 

time: 984 us -> 882 us (0.90)
  blocking collectives: 691 us -> 600 us
    psum x6 -> x12, blocking collectives: 246 us -> 155 us  [the longest x6 103 us: smoothed_terms(): lax.psum(lax.psum((jnp.sum(residual * precond), jnp.sum(precond * smooth)...]
    ppermute x24, starting transfers between devices: 58.6 us -> 37.5 us  [padded_2(): lax.ppermute(lax.slice_in_dim(block, 0, width, axis=dim), axis, backward)]
    ppermute x24, starting transfers between devices: 38.3 us -> 52.6 us  [padded_2(): lax.ppermute(lax.slice_in_dim(block, block.shape[dim] - width, None, axis...]
  transfers between devices with their start and end apart: 50 -> 50, of which waited for: 25 -> 24; matrix products, arithmetic and copies ran while one was open for 0% -> 0% of each run, Pallas kernels for 0% -> 0%
where the time goes in v1:
time: 882 us; the launch traced here: 879 us
  blocking collectives  600 us (68%)
  starting transfers between devices  95.2 us (11%)
  waiting for transfers between devices  77.2 us (9%)
  other arithmetic  55.2 us (6%)
  between operations  38.9 us (4%)
  local copies, waits for them, and re-layouts  12.8 us (1%)
    psum x5, blocking collectives, body(): lax.psum(jnp.sum(res_new * image, axis=(1, 2)), ('lat', 'lon'))  205 us
    psum x5, blocking collectives, body(): lax.psum(jnp.sum(dir_bar * inner_dir, axis=(1, 2)), ('lat', 'lon'))  200 us
    psum x6, blocking collectives, smoothed_terms(): lax.psum(lax.psum((jnp.sum(residual * precond), jnp.sum(precond * smooth)...  103 us
    ppermute x24, starting transfers between devices, padded_2(): lax.ppermute(lax.slice_in_dim(block, block.shape[dim] - width, None, axis...  52.6 us
    psum x6, blocking collectives, smoothed_terms(): lax.psum((jnp.sum(residual * precond), jnp.sum(precond * smooth)), 'lat')  51.9 us
    ppermute x24, waiting for transfers between devices, padded_2(): lax.ppermute(lax.slice_in_dim(block, 0, width, axis=dim), axis, backward)  46.3 us
    psum x1, blocking collectives, body(): lax.psum(jnp.stack([jnp.sum(cost_weights * padded_dirs[step][1:-1, 1:-1],...  39.1 us
    ppermute x24, starting transfers between devices, padded_2(): lax.ppermute(lax.slice_in_dim(block, 0, width, axis=dim), axis, backward)  37.5 us
  transfers between devices with their start and end apart: 50, of which 24 were waited for; matrix products, arithmetic and copies ran while one was open for 0% of the time, Pallas kernels for 0%

profile of v1, /device:TPU:31, one launch (start us, length us, event | category | flops | bytes accessed | tf_op | source)
XLA Modules:
  0.0 878.8 jit_solution(13837184558350917533)
XLA Ops:
  30.8 8.6 all-reduce.11
  39.4 17.2 %all-reduce.5 = (f32[]{:T(128)}, f32[]{:T(128)}) all-reduce(f32[]{:T(128)} %get-tuple-element.43, f32[]{:T(128)} %get-tuple-element.44), channel_id=1, replica_groups=mesh['lat'=4,'lon'=8] {'lon'}, use_global_device_ids=true, to_apply=%region_2.0 | all-reduce | flops 2 | bytes 16 | tf_op jit(solution)/shard_map/psum | solution.py:67
  70.9 8.6 all-reduce.10
  79.5 17.2 %all-reduce.4 = (f32[]{:T(128)}, f32[]{:T(128)}) all-reduce(f32[]{:T(128)} %get-tuple-element.41, f32[]{:T(128)} %get-tuple-element.42), channel_id=1, replica_groups=mesh['lat'=4,'lon'=8] {'lon'}, use_global_device_ids=true, to_apply=%region_8.0 | all-reduce | flops 2 | bytes 16 | tf_op jit(solution)/shard_map/psum | solution.py:67
  114.3 8.6 all-reduce.9
  123.0 17.3 %all-reduce.3 = (f32[]{:T(128)}, f32[]{:T(128)}) all-reduce(f32[]{:T(128)} %get-tuple-element.39, f32[]{:T(128)} %get-tuple-element.40), channel_id=1, replica_groups=mesh['lat'=4,'lon'=8] {'lon'}, use_global_device_ids=true, to_apply=%region_14.0 | all-reduce | flops 2 | bytes 16 | tf_op jit(solution)/shard_map/psum | solution.py:67
  157.3 8.6 all-reduce.8
  165.9 17.2 %all-reduce.2 = (f32[]{:T(128)}, f32[]{:T(128)}) all-reduce(f32[]{:T(128)} %get-tuple-element.37, f32[]{:T(128)} %get-tuple-element.38), channel_id=1, replica_groups=mesh['lat'=4,'lon'=8] {'lon'}, use_global_device_ids=true, to_apply=%region_20.0 | all-reduce | flops 2 | bytes 16 | tf_op jit(solution)/shard_map/psum | solution.py:67
  200.1 8.6 all-reduce.7
  208.7 17.2 %all-reduce.1 = (f32[]{:T(128)}, f32[]{:T(128)}) all-reduce(f32[]{:T(128)} %get-tuple-element.35, f32[]{:T(128)} %get-tuple-element.36), channel_id=1, replica_groups=mesh['lat'=4,'lon'=8] {'lon'}, use_global_device_ids=true, to_apply=%region_26.0 | all-reduce | flops 2 | bytes 16 | tf_op jit(solution)/shard_map/psum | solution.py:67
  242.7 8.6 all-reduce.6
  251.3 17.2 %all-reduce = (f32[]{:T(128)}, f32[]{:T(128)}) all-reduce(f32[]{:T(128)} %get-tuple-element.33, f32[]{:T(128)} %get-tuple-element.34), channel_id=1, replica_groups=mesh['lat'=4,'lon'=8] {'lon'}, use_global_device_ids=true, to_apply=%region_32.0 | all-reduce | flops 2 | bytes 16 | tf_op jit(solution)/shard_map/psum | solution.py:67
  276.8 39.1 %psum.269 = f32[6,8]{1,0:T(8,128)S(1)} all-reduce(f32[6,8]{1,0:T(8,128)S(1)} %stack.43), channel_id=1, replica_groups=mesh['lat'=4,'lon'=8] {'lat','lon'}, use_global_device_ids=true, to_apply=%region_42.0 | all-reduce | flops 48 | bytes 384 | tf_op jit(solution)/shard_map/psum | solution.py:116
  318.1 40.7 %psum.270 = f32[8]{0:T(128)S(1)} all-reduce(f32[8]{0:T(128)S(1)} %multiply_reduce_fusion.9), channel_id=1, replica_groups=mesh['lat'=4,'lon'=8] {'lat','lon'}, use_global_device_ids=true, to_apply=%region_44.0 | all-reduce | flops 8 | bytes 64 | tf_op jit(solution)/shard_map/psum | solution.py:146
  360.3 39.2 %psum.271 = f32[8]{0:T(128)S(1)} all-reduce(f32[8]{0:T(128)S(1)} %get-tuple-element.73), channel_id=1, replica_groups=mesh['lat'=4,'lon'=8] {'lat','lon'}, use_global_device_ids=true, to_apply=%region_46.0 | all-reduce | flops 8 | bytes 64 | tf_op jit(solution)/shard_map/psum | solution.py:149
  421.1 41.8 %psum.272 = f32[8]{0:T(128)S(1)} all-reduce(f32[8]{0:T(128)S(1)} %copy-done.109), channel_id=1, replica_groups=mesh['lat'=4,'lon'=8] {'lat','lon'}, use_global_device_ids=true, to_apply=%region_48.0 | all-reduce | flops 8 | bytes 64 | tf_op jit(solution)/shard_map/psum | solution.py:146
  465.1 41.1 %psum.273 = f32[8]{0:T(128)S(1)} all-reduce(f32[8]{0:T(128)S(1)} %get-tuple-element.67), channel_id=1, replica_groups=mesh['lat'=4,'lon'=8] {'lat','lon'}, use_global_device_ids=true, to_apply=%region_50.0 | all-reduce | flops 8 | bytes 64 | tf_op jit(solution)/shard_map/psum | solution.py:149
  528.4 40.2 %psum.274 = f32[8]{0:T(128)} all-reduce(f32[8]{0:T(128)} %get-tuple-element.65), channel_id=1, replica_groups=mesh['lat'=4,'lon'=8] {'lat','lon'}, use_global_device_ids=true, to_apply=%region_52.0 | all-reduce | flops 8 | bytes 64 | tf_op jit(solution)/shard_map/psum | solution.py:146
  574.1 41.3 %psum.275 = f32[8]{0:T(128)S(1)} all-reduce(f32[8]{0:T(128)S(1)} %copy-done.108), channel_id=1, replica_groups=mesh['lat'=4,'lon'=8] {'lat','lon'}, use_global_device_ids=true, to_apply=%region_54.0 | all-reduce | flops 8 | bytes 64 | tf_op jit(solution)/shard_map/psum | solution.py:149
  641.6 38.3 %psum.276 = f32[8]{0:T(128)S(1)} all-reduce(f32[8]{0:T(128)S(1)} %copy-done.110), channel_id=1, replica_groups=mesh['lat'=4,'lon'=8] {'lat','lon'}, use_global_device_ids=true, to_apply=%region_56.0 | all-reduce | flops 8 | bytes 64 | tf_op jit(solution)/shard_map/psum | solution.py:146
  683.9 41.5 %psum.277 = f32[8]{0:T(128)S(1)} all-reduce(f32[8]{0:T(128)S(1)} %get-tuple-element.55), channel_id=1, replica_groups=mesh['lat'=4,'lon'=8] {'lat','lon'}, use_global_device_ids=true, to_apply=%region_58.0 | all-reduce | flops 8 | bytes 64 | tf_op jit(solution)/shard_map/psum | solution.py:149
  751.8 38.9 %psum.278 = f32[8]{0:T(128)} all-reduce(f32[8]{0:T(128)} %get-tuple-element.53), channel_id=1, replica_groups=mesh['lat'=4,'lon'=8] {'lat','lon'}, use_global_device_ids=true, to_apply=%region_60.0 | all-reduce | flops 8 | bytes 64 | tf_op jit(solution)/shard_map/psum | solution.py:146
  796.0 42.2 %psum.279 = f32[8]{0:T(128)} all-reduce(f32[8]{0:T(128)} %get-tuple-element.49), channel_id=1, replica_groups=mesh['lat'=4,'lon'=8] {'lat','lon'}, use_global_device_ids=true, to_apply=%region_62.0 | all-reduce | flops 8 | bytes 64 | tf_op jit(solution)/shard_map/psum | solution.py:149
  844.6 6.8 collective-permute-done.44
  (404 shorter events, 233.6 us)
Async XLA Ops:
  2.2 5.8 collective-permute-start.1
  58.0 5.7 collective-permute-start.8
  101.5 5.7 collective-permute-start.12
  101.5 5.7 collective-permute-start.13
  144.5 5.7 collective-permute-start.16
  187.2 5.7 collective-permute-start.20
  229.9 5.7 collective-permute-start.24
  400.8 9.0 %collective-permute-start.28 = (f32[8,64,1]{2,1,0:T(8,128)S(1)}, f32[8,64,1]{2,1,0:T(8,128)S(1)}, u32[]{:S(2)}, u32[]{:S(2)}) collective-permute-start(f32[8,64,1]{2,1,0:T(8,128)S(1)} %get-tuple-element.126), channel_id=1, source_target_pairs={{1,0},{2,1},{3,2},{4,3},{5,4},{6,5},{7,6},{0,7},{9,8},{10,9},{11,1... | collective-permute-start | bytes 6152 | tf_op jit(solution)/shard_map/ppermute | solution.py:19
  402.4 7.4 collective-permute-start.29
  409.9 6.6 collective-permute-start.30
  507.5 10.0 %collective-permute-start.32 = (f32[8,64,1]{2,1,0:T(8,128)S(1)}, f32[8,64,1]{2,1,0:T(8,128)S(1)}, u32[]{:S(2)}, u32[]{:S(2)}) collective-permute-start(f32[8,64,1]{2,1,0:T(8,128)S(1)} %get-tuple-element.124), channel_id=1, source_target_pairs={{1,0},{2,1},{3,2},{4,3},{5,4},{6,5},{7,6},{0,7},{9,8},{10,9},{11,1... | collective-permute-start | bytes 6152 | tf_op jit(solution)/shard_map/ppermute | solution.py:19
  508.4 9.0 %collective-permute-start.33 = (f32[8,64,1]{2,1,0:T(8,128)S(1)}, f32[8,64,1]{2,1,0:T(8,128)S(1)}, u32[]{:S(2)}, u32[]{:S(2)}) collective-permute-start(f32[8,64,1]{2,1,0:T(8,128)S(1)} %get-tuple-element.123), channel_id=1, source_target_pairs={{0,1},{1,2},{2,3},{3,4},{4,5},{5,6},{6,7},{7,0},{8,9},{9,10},{10,1... | collective-permute-start | bytes 6152 | tf_op jit(solution)/shard_map/ppermute | solution.py:16
  518.3 6.8 collective-permute-start.34
  617.7 10.4 %collective-permute-start.36 = (f32[8,64,1]{2,1,0:T(8,128)S(1)}, f32[8,64,1]{2,1,0:T(8,128)S(1)}, u32[]{:S(2)}, u32[]{:S(2)}) collective-permute-start(f32[8,64,1]{2,1,0:T(8,128)S(1)} %get-tuple-element.122), channel_id=1, source_target_pairs={{1,0},{2,1},{3,2},{4,3},{5,4},{6,5},{7,6},{0,7},{9,8},{10,9},{11,1... | collective-permute-start | bytes 6152 | tf_op jit(solution)/shard_map/ppermute | solution.py:19
  618.8 9.3 %collective-permute-start.37 = (f32[8,64,1]{2,1,0:T(8,128)S(1)}, f32[8,64,1]{2,1,0:T(8,128)S(1)}, u32[]{:S(2)}, u32[]{:S(2)}) collective-permute-start(f32[8,64,1]{2,1,0:T(8,128)S(1)} %get-tuple-element.121), channel_id=1, source_target_pairs={{0,1},{1,2},{2,3},{3,4},{4,5},{5,6},{6,7},{7,0},{8,9},{9,10},{10,1... | collective-permute-start | bytes 6152 | tf_op jit(solution)/shard_map/ppermute | solution.py:16
  628.8 7.4 collective-permute-start.38
  727.8 10.3 %collective-permute-start.40 = (f32[8,64,1]{2,1,0:T(8,128)S(1)}, f32[8,64,1]{2,1,0:T(8,128)S(1)}, u32[]{:S(2)}, u32[]{:S(2)}) collective-permute-start(f32[8,64,1]{2,1,0:T(8,128)S(1)} %get-tuple-element.120), channel_id=1, source_target_pairs={{1,0},{2,1},{3,2},{4,3},{5,4},{6,5},{7,6},{0,7},{9,8},{10,9},{11,1... | collective-permute-start | bytes 6152 | tf_op jit(solution)/shard_map/ppermute | solution.py:19
  728.9 9.2 %collective-permute-start.41 = (f32[8,64,1]{2,1,0:T(8,128)S(1)}, f32[8,64,1]{2,1,0:T(8,128)S(1)}, u32[]{:S(2)}, u32[]{:S(2)}) collective-permute-start(f32[8,64,1]{2,1,0:T(8,128)S(1)} %get-tuple-element.119), channel_id=1, source_target_pairs={{0,1},{1,2},{2,3},{3,4},{4,5},{5,6},{6,7},{7,0},{8,9},{9,10},{10,1... | collective-permute-start | bytes 6152 | tf_op jit(solution)/shard_map/ppermute | solution.py:16
  738.9 9.3 %collective-permute-start.42 = (f32[8,1,258]{2,1,0:T(1,128)}, f32[8,1,258]{2,1,0:T(1,128)}, u32[]{:S(2)}, u32[]{:S(2)}) collective-permute-start(f32[8,1,258]{2,1,0:T(1,128)} %get-tuple-element.109), channel_id=1, source_target_pairs={{8,0},{16,8},{24,16},{9,1},{17,9},{25,17},{10,2},{18,10},{26,18},{... | collective-permute-start | bytes 24776 | tf_op jit(solution)/shard_map/ppermute | solution.py:19
  742.3 5.9 collective-permute-start.43
  841.0 10.4 %collective-permute-start.44 = (f32[8,64,1]{2,1,0:T(8,128)S(1)}, f32[8,64,1]{2,1,0:T(8,128)S(1)}, u32[]{:S(2)}, u32[]{:S(2)}) collective-permute-start(f32[8,64,1]{2,1,0:T(8,128)S(1)} %get-tuple-element.118), channel_id=1, source_target_pairs={{1,0},{2,1},{3,2},{4,3},{5,4},{6,5},{7,6},{0,7},{9,8},{10,9},{11,1... | collective-permute-start | bytes 6152 | tf_op jit(solution)/shard_map/ppermute | solution.py:19
  842.1 9.3 %collective-permute-start.45 = (f32[8,64,1]{2,1,0:T(8,128)S(1)}, f32[8,64,1]{2,1,0:T(8,128)S(1)}, u32[]{:S(2)}, u32[]{:S(2)}) collective-permute-start(f32[8,64,1]{2,1,0:T(8,128)S(1)} %get-tuple-element.117), channel_id=1, source_target_pairs={{0,1},{1,2},{2,3},{3,4},{4,5},{5,6},{6,7},{7,0},{8,9},{9,10},{10,1... | collective-permute-start | bytes 6152 | tf_op jit(solution)/shard_map/ppermute | solution.py:16
  861.2 14.5 %collective-permute-start.49 = (f32[8,1,256]{2,1,0:T(1,128)S(1)}, f32[8,1,256]{2,1,0:T(1,128)S(1)}, u32[]{:S(2)}, u32[]{:S(2)}) collective-permute-start(f32[8,1,256]{2,1,0:T(1,128)S(1)} %slice.651), channel_id=1, source_target_pairs={{8,0},{16,8},{24,16},{9,1},{17,9},{25,17},{10,2},{18,10},{26,18},{... | collective-permute-start | bytes 24584 | tf_op jit(solution)/shard_map/ppermute | solution.py:33
  865.1 7.8 collective-permute-start.48
  (137 other events, 4538.8 us)
